TPU v7x, 32 devices: a whole 2x2x4 slice. The times are simulated.
32 devices in a mesh: gx: 2 (over core), gy: 16 (over z, y, x).
Axes of the slice: x: 2, y: 2, z: 4, core: 2. Of those that a mesh axis runs over, the one named last changes fastest.
Arguments:
- data: float32 [32, 256, 128], P('gx', 'gy'), may hold values from -6 to 6
- precond: float32 [32, 256, 128], P('gx', 'gy'), may hold values from 0.5 to 2
- psf: float32 [2, 16, 17, 17, 17], P('gx', 'gy'), may hold values from -0.05 to 0.05
Outputs:
- model: float32 [32, 256, 128], P('gx', 'gy')
- residual: float32 [32, 256, 128], P('gx', 'gy')
All inputs are finite; a program needn't handle non-finite values.
Results may differ from a plain program's by a relative error of at most 0.0003.
Values sent between devices are 32-bit elements; how exact they have to be, the bound alone decides.
A program may use at most 64 MiB of HBM per device.

v0:
```python
import functools
import math

import jax
import jax.numpy as jnp
import numpy as np
from jax import lax
from jax.experimental import pallas as pl
from jax.experimental.pallas import tpu as pltpu
from jax.sharding import PartitionSpec as P

ITERS = 2
relaxation = 0.7
exact = lax.Precision.HIGHEST
LANES = 128
SUB = 8


def times_phase(value, turn, size, sign):
    if value is None:
        return None
    re, im = value
    turn = (sign * turn) % size
    eighth = 8 * turn
    if eighth == 0:
        return value
    if eighth == 2 * size:
        return (-im, re)
    if eighth == 4 * size:
        return (-re, -im)
    if eighth == 6 * size:
        return (im, -re)
    angle = 2.0 * math.pi * turn / size
    cosine, sine = math.cos(angle), math.sin(angle)
    if eighth % size == 0:
        root = math.sqrt(0.5)
        first, second = (re - im) * root, (re + im) * root
        if eighth == size:
            return (first, second)
        if eighth == 3 * size:
            return (-second, first)
        if eighth == 5 * size:
            return (-first, -second)
        return (second, -first)
    return (re * cosine - im * sine, re * sine + im * cosine)


def plus(a, b):
    if a is None:
        return b
    if b is None:
        return a
    return (a[0] + b[0], a[1] + b[1])


def minus(a, b):
    if b is None:
        return a
    if a is None:
        return (-b[0], -b[1])
    return (a[0] - b[0], a[1] - b[1])


def transform(values, sign, wanted):
    size = len(values)
    if all(v is None for v in values):
        return [None] * wanted
    if size == 1:
        return list(values)
    half = size // 2
    if size % 2:
        raise ValueError("length")
    even = transform(values[0::2], sign, min(half, wanted))
    odd = transform(values[1::2], sign, min(half, wanted))
    odd = [times_phase(v, k, size, sign) for k, v in enumerate(odd)]
    low = [plus(a, b) for a, b in zip(even, odd)]
    high = [minus(a, b) for a, b in zip(even, odd)]
    return (low + high)[:wanted]


def tables(depth, width):
    half = width // 2
    length = depth + 2 * half
    count = length // 2 + 1
    k = np.arange(count)
    field = np.zeros((depth, 2 * LANES))
    turns = (np.arange(depth)[:, None] + half) * k[None, :] % length
    angle = turns * (2.0 * np.pi / length)
    field[:, :count] = np.cos(angle)
    field[:, LANES : LANES + count] = -np.sin(angle)
    kernel = np.zeros((LANES, 2 * LANES))
    angle = np.arange(width)[:, None] * k[None, :] % length * (2.0 * np.pi / length)
    kernel[:width, :count] = np.cos(angle)
    kernel[:width, LANES : LANES + count] = np.sin(angle)
    back = np.zeros((2 * LANES, depth))
    weight = np.where((k == 0) | (2 * k == length), 1.0, 2.0) / length
    angle = k[:, None] * np.arange(depth)[None, :] % length * (2.0 * np.pi / length)
    back[:count] = weight[:, None] * np.cos(angle)
    back[LANES : LANES + count] = -weight[:, None] * np.sin(angle)
    return field.astype(np.float32), kernel.astype(np.float32), back


def spectra_kernel(width, region_x, region_y, rows, psf_ref, table_ref, g_ref, k1r, k1i, k2r, k2i):
    for b in range(width):
        both = jnp.dot(
            psf_ref[pl.ds(b * rows, rows), :], table_ref[...],
            precision=exact, preferred_element_type=jnp.float32,
        )
        k1r[pl.ds(b * rows, rows), :] = both[:, :LANES]
        k1i[pl.ds(b * rows, rows), :] = both[:, LANES:]

    @pl.loop(0, rows // SUB)
    def _(tile):
        at = lambda i: pl.ds(pl.multiple_of(i * rows + tile * SUB, SUB), SUB)
        values = [(k1r[at(b), :], k1i[at(b), :]) for b in range(width)]
        values += [None] * (region_y - width)
        for ky, (re, im) in enumerate(transform(values, 1, region_y)):
            k2r[at(ky), :] = re
            k2i[at(ky), :] = im

    @pl.loop(0, 4)
    def _(node):
        @pl.loop(0, region_y // SUB)
        def _(tile):
            at = lambda a: pl.ds(tile * SUB * rows + node * width + a, SUB, stride=rows)
            values = [(k2r[at(a), :], k2i[at(a), :]) for a in range(width)]
            values += [None] * (region_x - width)
            for kx, (re, im) in enumerate(transform(values, 1, region_x)):
                to = pl.ds(pl.multiple_of(kx * region_y + tile * SUB, SUB), SUB)
                g_ref[node, 0, to, :] = re
                g_ref[node, 1, to, :] = im


def apply_kernel(
    count_x, count_y, half,
    region_ref, data_ref, precond_ref, g_hbm, field_ref, back_ref,
    model_ref, residual_ref,
    g_ref, zr, zi, yr, yi, vx, ur, ui, w_ref, o_ref, sem,
):
    region_x, region_y = count_x + 2 * half, count_y + 2 * half
    fetch = pltpu.make_async_copy(g_hbm, g_ref, sem)
    fetch.start()
    block = 128
    for start in range(0, region_x * region_y, block):
        both = jnp.dot(
            region_ref[pl.ds(start, block), :], field_ref[...],
            precision=exact, preferred_element_type=jnp.float32,
        )
        zr[pl.ds(start, block), :] = both[:, :LANES]
        zi[pl.ds(start, block), :] = both[:, LANES:]

    @pl.loop(0, region_x // SUB)
    def _(tile):
        at = lambda y: pl.ds(tile * SUB * region_y + y, SUB, stride=region_y)
        values = [(zr[at(y), :], zi[at(y), :]) for y in range(region_y)]
        for ky, (re, im) in enumerate(transform(values, -1, region_y)):
            to = pl.ds(pl.multiple_of(ky * region_x + tile * SUB, SUB), SUB)
            yr[to, :] = re
            yi[to, :] = im

    fetch.wait()

    @pl.loop(0, region_y // SUB)
    def _(tile):
        at = lambda x: pl.ds(tile * SUB * region_x + x, SUB, stride=region_x)
        values = [(yr[at(x), :], yi[at(x), :]) for x in range(region_x)]
        for kx, (re, im) in enumerate(transform(values, -1, region_x)):
            vx[0, kx] = re
            vx[1, kx] = im

        @pl.loop(0, 2)
        def _(j):
            parts = []
            for i in range(2):
                values = []
                for kx in range(region_x):
                    to = pl.ds(pl.multiple_of(kx * region_y + tile * SUB, SUB), SUB)
                    gr, gi = g_ref[2 * j + i, 0, to, :], g_ref[2 * j + i, 1, to, :]
                    vr, vi = vx[0, kx], vx[1, kx]
                    values.append((vr * gr - vi * gi, vr * gi + vi * gr))
                parts.append(transform(values, 1, count_x))
            for x in range(count_x):
                s = (x + 0.5) / count_x
                to = pl.ds(pl.multiple_of(x * region_y + tile * SUB, SUB), SUB)
                (ar, ai), (br, bi) = parts[0][x], parts[1][x]
                ur[j, to, :] = (1.0 - s) * ar + s * br
                ui[j, to, :] = (1.0 - s) * ai + s * bi

    @pl.loop(0, count_x // SUB)
    def _(tile):
        parts = []
        for j in range(2):
            at = lambda ky: pl.ds(tile * SUB * region_y + ky, SUB, stride=region_y)
            values = [(ur[j, at(ky), :], ui[j, at(ky), :]) for ky in range(region_y)]
            parts.append(transform(values, 1, count_y))
        for y in range(count_y):
            t = (y + 0.5) / count_y
            to = pl.ds(pl.multiple_of(y * count_x + tile * SUB, SUB), SUB)
            (ar, ai), (br, bi) = parts[0][y], parts[1][y]
            w_ref[to, :LANES] = (1.0 - t) * ar + t * br
            w_ref[to, LANES:] = (1.0 - t) * ai + t * bi

    o_ref[...] = jnp.dot(
        w_ref[...], back_ref[...], precision=exact, preferred_element_type=jnp.float32
    )
    for x in range(count_x):
        blended = o_ref[pl.ds(x, count_y, stride=count_x), :]
        model = region_ref[pl.ds((x + half) * region_y + half, count_y), :]
        residual = data_ref[x] - (model + blended)
        residual_ref[x] = residual
        model_ref[x] = model + relaxation * precond_ref[x] * residual


def padded_2(shard, sides, width):
    for axis, dim in sides:
        size, length = (lax.axis_size(axis), shard.shape[dim])
        up = [(i, (i + 1) % size) for i in range(size - 1)]
        down = [(j, i) for i, j in up]
        last = lax.slice_in_dim(shard, length - width, length, axis=dim)
        leading = lax.slice_in_dim(shard, 0, width, axis=dim)
        before = lax.ppermute(last, axis, up)
        after = lax.ppermute(leading, axis, down)
        shard = jnp.concatenate([before, shard, after], axis=dim)
    return shard


def passed_along(shard, axis, by):
    length = lax.axis_size(axis)
    pairs = [(i, i + by) for i in range(length) if 0 <= i + by < length]
    return lax.ppermute(shard, axis, pairs)


def node_kernels(psf):
    own = psf[0, 0]
    last_inline = lax.axis_index("gx") == lax.axis_size("gx") - 1
    last_crossline = lax.axis_index("gy") == lax.axis_size("gy") - 1
    inline = jnp.where(last_inline, own, passed_along(own, "gx", -1))
    pair = jnp.stack([own, inline])
    crossline = jnp.where(last_crossline, pair, passed_along(pair, "gy", -1))
    return jnp.concatenate([pair, crossline])


def local(data, precond, psf):
    count_x, count_y, depth = data.shape
    width = psf.shape[2]
    half = width // 2
    region_x, region_y = count_x + 2 * half, count_y + 2 * half
    field, kernel, back = tables(depth, width)
    back = (back / (region_x * region_y)).astype(np.float32)
    f32 = jnp.float32

    model = precond * data
    nodes = node_kernels(psf)
    rows = -(-4 * width // SUB) * SUB
    arranged = nodes.transpose(2, 0, 1, 3).reshape(width, 4 * width, width)
    arranged = jnp.pad(arranged, ((0, 0), (0, rows - 4 * width), (0, LANES - width)))
    arranged = arranged.reshape(width * rows, LANES)
    spectra = pl.pallas_call(
        functools.partial(spectra_kernel, width, region_x, region_y, rows),
        out_shape=jax.ShapeDtypeStruct((4, 2, region_x * region_y, LANES), f32),
        scratch_shapes=[pltpu.VMEM((width * rows, LANES), f32)] * 2
        + [pltpu.VMEM((region_y * rows, LANES), f32)] * 2,
        compiler_params=pltpu.CompilerParams(vmem_limit_bytes=24 << 20),
        cost_estimate=pl.CostEstimate(flops=10**9, bytes_accessed=10**6, transcendentals=0),
        name="spectra",
    )(arranged, kernel)

    vmem = pl.BlockSpec(memory_space=pltpu.VMEM)
    apply = pl.pallas_call(
        functools.partial(apply_kernel, count_x, count_y, half),
        out_shape=[jax.ShapeDtypeStruct(data.shape, f32)] * 2,
        in_specs=[vmem, vmem, vmem, pl.BlockSpec(memory_space=pl.ANY), vmem, vmem],
        scratch_shapes=[
            pltpu.VMEM((4, 2, region_x * region_y, LANES), f32),
            pltpu.VMEM((region_x * region_y, LANES), f32),
            pltpu.VMEM((region_x * region_y, LANES), f32),
            pltpu.VMEM((region_x * region_y, LANES), f32),
            pltpu.VMEM((region_x * region_y, LANES), f32),
            pltpu.VMEM((2, region_x, SUB, LANES), f32),
            pltpu.VMEM((2, count_x * region_y, LANES), f32),
            pltpu.VMEM((2, count_x * region_y, LANES), f32),
            pltpu.VMEM((count_x * count_y, 2 * LANES), f32),
            pltpu.VMEM((count_x * count_y, LANES), f32),
            pltpu.SemaphoreType.DMA,
        ],
        compiler_params=pltpu.CompilerParams(vmem_limit_bytes=24 << 20),
        name="apply",
    )
    residual = data
    for sweep_index in range(ITERS):
        region = padded_2(model, (("gx", 0), ("gy", 1)), half)
        region = region.reshape(region_x * region_y, depth)
        model, residual = apply(region, data, precond, spectra, field, back)
    return model, residual


def solution(mesh):
    placed = (P("gx", "gy", None), P("gx", "gy", None), P("gx", "gy", None, None, None))
    return jax.shard_map(
        local,
        mesh=mesh,
        in_specs=placed,
        out_specs=(P("gx", "gy", None), P("gx", "gy", None)),
        check_vma=False,
    )
```

profile of v0, /device:TPU:0, one launch (start us, length us, event | category | flops | bytes accessed | tf_op | source)
XLA Modules:
  0.0 63.7 jit_solution(3056233879400979031)
XLA Ops:
  0.6 1.0 %copy.18 = f32[1,1,17,17,17]{4,3,1,2,0:T(8,128)S(1)} copy(f32[1,1,17,17,17]{4,1,3,2,0:T(1,128)} %param.8) | data formatting | bytes 39304
  1.6 1.3 %collective-permute-start.4 = (f32[17,17,17]{2,1,0:T(8,128)S(1)}, f32[17,17,17]{2,1,0:T(8,128)S(1)}, u32[]{:S(2)}, u32[]{:S(2)}) collective-permute-start(f32[17,17,17]{2,1,0:T(8,128)S(1)} %bitcast.17), channel_id=1, source_target_pairs={{16,0},{17,1},{18,2},{19,3},{20,4},{21,5},{22,6},{23,7},{24,8},{25... | collective-permute-start | bytes 58964 | tf_op jit(solution)/shard_map/ppermute | solution.py:230
  2.9 1.0 %mul.3 = f32[16,16,128]{2,1,0:T(8,128)S(1)} multiply(f32[16,16,128]{2,1,0:T(8,128)} %precond_ref.3, f32[16,16,128]{2,1,0:T(8,128)} %data_ref.3) | non-fusion elementwise | flops 32768 | bytes 393216 | tf_op jit(solution)/shard_map/mul | solution.py:252
  3.9 1.1 %collective-permute-done.4 = f32[17,17,17]{2,1,0:T(8,128)S(1)} collective-permute-done((f32[17,17,17]{2,1,0:T(8,128)S(1)}, f32[17,17,17]{2,1,0:T(8,128)S(1)}, u32[]{:S(2)}, u32[]{:S(2)}) %collective-permute-start.4) | collective-permute-done | bytes 19684 | tf_op jit(solution)/shard_map/ppermute | solution.py:230
  5.0 0.9 %broadcast_select_fusion.1 = f32[17,17,17]{2,1,0:T(8,128)S(1)} fusion(f32[17,17,17]{2,1,0:T(8,128)S(1)} %collective-permute-done.4, pred[]{:T(512)S(6)} %eq.6, f32[1,1,17,17,17]{4,1,3,2,0:T(1,128)} %param.8), kind=kLoop, calls=%fused_computation.7 | loop fusion | flops 4913 | bytes 58957 | tf_op jit(solution)/shard_map/jit(_where)/select_n | solution.py:237
  5.9 0.0 copy-start.4
  5.9 0.1 stack.6
  6.0 1.2 %pad_maximum_fusion.2 = f32[2,17,17,17]{3,0,2,1:T(2,128)S(1)} fusion(f32[1,17,17,17]{3,0,2,1:T(1,128)S(1)} %stack.6, f32[1,17,17,17]{3,0,2,1:T(1,128)} %bitcast.14), kind=kLoop, calls=%fused_computation.3 | loop fusion | flops 9826 | bytes 78608 | tf_op jit(solution)/shard_map/stack | solution.py:238
  7.3 1.3 %collective-permute-start.5 = (f32[2,17,17,17]{3,0,2,1:T(2,128)S(1)}, f32[2,17,17,17]{3,0,2,1:T(2,128)S(1)}, u32[]{:S(2)}, u32[]{:S(2)}) collective-permute-start(f32[2,17,17,17]{3,0,2,1:T(2,128)S(1)} %pad_maximum_fusion.2), channel_id=1, source_target_pairs={{1,0},{2,1},{3,2},{4,3},{5,4},{6,5},{7,6},{8,7},{9,8},{10,9},{11,1... | collective-permute-start | bytes 117920 | tf_op jit(solution)/shard_map/ppermute | solution.py:230
  8.6 2.0 %collective-permute-start = (f32[8,16,128]{2,1,0:T(8,128)S(1)}, f32[8,16,128]{2,1,0:T(8,128)S(1)}, u32[]{:S(2)}, u32[]{:S(2)}) collective-permute-start(f32[8,16,128]{2,1,0:T(8,128)S(1)} %get-tuple-element.10), channel_id=1, source_target_pairs={{0,16},{1,17},{2,18},{3,19},{4,20},{5,21},{6,22},{7,23},{8,24},{9,... | collective-permute-start | bytes 196616 | tf_op jit(solution)/shard_map/ppermute | solution.py:221
  10.7 1.3 %collective-permute-start.1 = (f32[8,16,128]{2,1,0:T(8,128)S(1)}, f32[8,16,128]{2,1,0:T(8,128)S(1)}, u32[]{:S(2)}, u32[]{:S(2)}) collective-permute-start(f32[8,16,128]{2,1,0:T(8,128)S(1)} %get-tuple-element.11), channel_id=1, source_target_pairs={{16,0},{17,1},{18,2},{19,3},{20,4},{21,5},{22,6},{23,7},{24,8},{25... | collective-permute-start | bytes 196616 | tf_op jit(solution)/shard_map/ppermute | solution.py:222
  12.0 7.5 %collective-permute-done.5 = f32[2,17,17,17]{3,0,2,1:T(2,128)S(1)} collective-permute-done((f32[2,17,17,17]{3,0,2,1:T(2,128)S(1)}, f32[2,17,17,17]{3,0,2,1:T(2,128)S(1)}, u32[]{:S(2)}, u32[]{:S(2)}) %collective-permute-start.5) | collective-permute-done | bytes 39336 | tf_op jit(solution)/shard_map/ppermute | solution.py:230
  19.5 1.3 %broadcast_select_fusion = f32[2,17,17,17]{3,0,2,1:T(2,128)S(1)} fusion(f32[2,17,17,17]{3,0,2,1:T(2,128)S(1)} %collective-permute-done.5, pred[]{:T(512)S(6)} %eq.7, f32[1,17,17,17]{3,0,2,1:T(1,128)S(1)} %stack.6, f32[1,17,17,17]{3,0,2,1:T(1,128)} %bitcast.15), kind=kLoop, calls=%fused_computation.4 | loop fusion | flops 19652 | bytes 117913 | tf_op jit(solution)/shard_map/jit(_where)/select_n | solution.py:239
  20.9 4.5 %collective-permute-start.2 = (f32[32,8,128]{2,1,0:T(8,128)S(1)}, f32[32,8,128]{2,1,0:T(8,128)S(1)}, u32[]{:S(2)}, u32[]{:S(2)}) collective-permute-start(f32[32,8,128]{2,1,0:T(8,128)S(1)} %get-tuple-element.6), channel_id=1, source_target_pairs={{0,1},{1,2},{2,3},{3,4},{4,5},{5,6},{6,7},{7,8},{8,9},{9,10},{10,1... | collective-permute-start | bytes 393224 | tf_op jit(solution)/shard_map/ppermute | solution.py:221
  25.4 1.3 %collective-permute-start.3 = (f32[32,8,128]{2,1,0:T(8,128)S(1)}, f32[32,8,128]{2,1,0:T(8,128)S(1)}, u32[]{:S(2)}, u32[]{:S(2)}) collective-permute-start(f32[32,8,128]{2,1,0:T(8,128)S(1)} %get-tuple-element.7), channel_id=1, source_target_pairs={{1,0},{2,1},{3,2},{4,3},{5,4},{6,5},{7,6},{8,7},{9,8},{10,9},{11,1... | collective-permute-start | bytes 393224 | tf_op jit(solution)/shard_map/ppermute | solution.py:222
  26.7 0.5 maximum_bitcast_fusion
  27.2 0.1 copy.13
  27.3 0.0 copy-start
  27.3 0.0 copy-start.2
  27.4 0.0 copy-start.3
  27.4 0.1 reshape.20
  27.5 3.3 %spectra.1.g_hbm = f32[4,2,1024,128]{3,2,1,0:T(8,128)S(1)} custom-call(f32[1224,128]{1,0:T(8,128)S(1)} %bitcast.11, f32[128,256]{1,0:T(8,128)S(1)} %copy-done.4), custom_call_target="tpu_custom_call" | custom-call | flops 1000000000 | bytes 1000000 | tf_op jit(solution)/shard_map/spectra/pallas_call | solution.py:258
  30.8 1.5 %collective-permute-done.3 = f32[32,8,128]{2,1,0:T(8,128)S(1)} collective-permute-done((f32[32,8,128]{2,1,0:T(8,128)S(1)}, f32[32,8,128]{2,1,0:T(8,128)S(1)}, u32[]{:S(2)}, u32[]{:S(2)}) %collective-permute-start.3) | collective-permute-done | bytes 131104 | tf_op jit(solution)/shard_map/ppermute | solution.py:222
  32.4 7.3 %apply.2 = (f32[16,16,128]{2,1,0:T(8,128)S(1)}, f32[16,16,128]{2,1,0:T(8,128)}) custom-call(f32[1024,128]{1,0:T(8,128)S(1)} %bitcast.13, f32[16,16,128]{2,1,0:T(8,128)S(1)} %copy-done.1, f32[16,16,128]{2,1,0:T(8,128)S(1)} %copy-done, f32[4,2,1024,128]{3,2,1,0:T(8,128)S(1)} %spectra.1.g_hbm, f32[128,256]{1,0:T(8,128)S(1)} %copy-done.3, f32[256,128]{1,0:T(8,128)S(1)} %copy-done.2), custom_call_target="tpu_custom_call" | custom-call | tf_op jit(solution)/shard_map/apply/pallas_call | solution.py:293
  39.7 1.3 %collective-permute-start.6 = (f32[8,16,128]{2,1,0:T(8,128)S(1)}, f32[8,16,128]{2,1,0:T(8,128)S(1)}, u32[]{:S(2)}, u32[]{:S(2)}) collective-permute-start(f32[8,16,128]{2,1,0:T(8,128)S(1)} %get-tuple-element.9), channel_id=1, source_target_pairs={{0,16},{1,17},{2,18},{3,19},{4,20},{5,21},{6,22},{7,23},{8,24},{9,... | collective-permute-start | bytes 196616 | tf_op jit(solution)/shard_map/ppermute | solution.py:221
  41.0 1.3 %collective-permute-start.7 = (f32[8,16,128]{2,1,0:T(8,128)S(1)}, f32[8,16,128]{2,1,0:T(8,128)S(1)}, u32[]{:S(2)}, u32[]{:S(2)}) collective-permute-start(f32[8,16,128]{2,1,0:T(8,128)S(1)} %get-tuple-element.8), channel_id=1, source_target_pairs={{16,0},{17,1},{18,2},{19,3},{20,4},{21,5},{22,6},{23,7},{24,8},{25... | collective-permute-start | bytes 196616 | tf_op jit(solution)/shard_map/ppermute | solution.py:222
  42.3 1.8 %collective-permute-done.7 = f32[8,16,128]{2,1,0:T(8,128)S(1)} collective-permute-done((f32[8,16,128]{2,1,0:T(8,128)S(1)}, f32[8,16,128]{2,1,0:T(8,128)S(1)}, u32[]{:S(2)}, u32[]{:S(2)}) %collective-permute-start.7) | collective-permute-done | bytes 65568 | tf_op jit(solution)/shard_map/ppermute | solution.py:222
  44.2 4.7 %collective-permute-start.8 = (f32[32,8,128]{2,1,0:T(8,128)S(1)}, f32[32,8,128]{2,1,0:T(8,128)S(1)}, u32[]{:S(2)}, u32[]{:S(2)}) collective-permute-start(f32[32,8,128]{2,1,0:T(8,128)S(1)} %get-tuple-element.4), channel_id=1, source_target_pairs={{0,1},{1,2},{2,3},{3,4},{4,5},{5,6},{6,7},{7,8},{8,9},{9,10},{10,1... | collective-permute-start | bytes 393224 | tf_op jit(solution)/shard_map/ppermute | solution.py:221
  48.8 1.3 %collective-permute-start.9 = (f32[32,8,128]{2,1,0:T(8,128)S(1)}, f32[32,8,128]{2,1,0:T(8,128)S(1)}, u32[]{:S(2)}, u32[]{:S(2)}) collective-permute-start(f32[32,8,128]{2,1,0:T(8,128)S(1)} %get-tuple-element.5), channel_id=1, source_target_pairs={{1,0},{2,1},{3,2},{4,3},{5,4},{6,5},{7,6},{8,7},{9,8},{10,9},{11,1... | collective-permute-start | bytes 393224 | tf_op jit(solution)/shard_map/ppermute | solution.py:222
  50.1 1.8 %collective-permute-done.8 = f32[32,8,128]{2,1,0:T(8,128)S(1)} collective-permute-done((f32[32,8,128]{2,1,0:T(8,128)S(1)}, f32[32,8,128]{2,1,0:T(8,128)S(1)}, u32[]{:S(2)}, u32[]{:S(2)}) %collective-permute-start.8) | collective-permute-done | bytes 131104 | tf_op jit(solution)/shard_map/ppermute | solution.py:221
  51.9 4.4 %collective-permute-done.9 = f32[32,8,128]{2,1,0:T(8,128)S(1)} collective-permute-done((f32[32,8,128]{2,1,0:T(8,128)S(1)}, f32[32,8,128]{2,1,0:T(8,128)S(1)}, u32[]{:S(2)}, u32[]{:S(2)}) %collective-permute-start.9) | collective-permute-done | bytes 131104 | tf_op jit(solution)/shard_map/ppermute | solution.py:222
  56.3 7.3 %apply.3 = (f32[16,16,128]{2,1,0:T(8,128)}, f32[16,16,128]{2,1,0:T(8,128)}) custom-call(f32[1024,128]{1,0:T(8,128)S(1)} %bitcast.12, f32[16,16,128]{2,1,0:T(8,128)S(1)} %copy-done.1, f32[16,16,128]{2,1,0:T(8,128)S(1)} %copy-done, f32[4,2,1024,128]{3,2,1,0:T(8,128)S(1)} %spectra.1.g_hbm, f32[128,256]{1,0:T(8,128)S(1)} %copy-done.3, f32[256,128]{1,0:T(8,128)S(1)} %copy-done.2), custom_call_target="tpu_custom_call" | custom-call | tf_op jit(solution)/shard_map/apply/pallas_call | solution.py:293
  (23 shorter events, 0.3 us)
Async XLA Ops:
  0.6 26.1 %copy-start.5 = (f32[1,1,17,17,17]{4,1,3,2,0:T(1,128)S(1)}, f32[1,1,17,17,17]{4,1,3,2,0:T(1,128)}, u32[]{:S(2)}) copy-start(f32[1,1,17,17,17]{4,1,3,2,0:T(1,128)} %param.8) | copy-start | bytes 58960
  1.6 3.4 %collective-permute-start.4 = (f32[17,17,17]{2,1,0:T(8,128)S(1)}, f32[17,17,17]{2,1,0:T(8,128)S(1)}, u32[]{:S(2)}, u32[]{:S(2)}) collective-permute-start(f32[17,17,17]{2,1,0:T(8,128)S(1)} %bitcast.17), channel_id=1, source_target_pairs={{16,0},{17,1},{18,2},{19,3},{20,4},{21,5},{22,6},{23,7},{24,8},{25... | collective-permute-start | bytes 58964 | tf_op jit(solution)/shard_map/ppermute | solution.py:230
  5.9 21.6 %copy-start.4 = (f32[128,256]{1,0:T(8,128)S(1)}, f32[128,256]{1,0:T(8,128)}, u32[]{:S(2)}) copy-start(f32[128,256]{1,0:T(8,128)} %constant.22.clone.table_ref) | copy-start | bytes 393220
  7.3 12.2 %collective-permute-start.5 = (f32[2,17,17,17]{3,0,2,1:T(2,128)S(1)}, f32[2,17,17,17]{3,0,2,1:T(2,128)S(1)}, u32[]{:S(2)}, u32[]{:S(2)}) collective-permute-start(f32[2,17,17,17]{3,0,2,1:T(2,128)S(1)} %pad_maximum_fusion.2), channel_id=1, source_target_pairs={{1,0},{2,1},{3,2},{4,3},{5,4},{6,5},{7,6},{8,7},{9,8},{10,9},{11,1... | collective-permute-start | bytes 117920 | tf_op jit(solution)/shard_map/ppermute | solution.py:230
  8.6 12.2 %collective-permute-start = (f32[8,16,128]{2,1,0:T(8,128)S(1)}, f32[8,16,128]{2,1,0:T(8,128)S(1)}, u32[]{:S(2)}, u32[]{:S(2)}) collective-permute-start(f32[8,16,128]{2,1,0:T(8,128)S(1)} %get-tuple-element.10), channel_id=1, source_target_pairs={{0,16},{1,17},{2,18},{3,19},{4,20},{5,21},{6,22},{7,23},{8,24},{9,... | collective-permute-start | bytes 196616 | tf_op jit(solution)/shard_map/ppermute | solution.py:221
  10.7 10.1 %collective-permute-start.1 = (f32[8,16,128]{2,1,0:T(8,128)S(1)}, f32[8,16,128]{2,1,0:T(8,128)S(1)}, u32[]{:S(2)}, u32[]{:S(2)}) collective-permute-start(f32[8,16,128]{2,1,0:T(8,128)S(1)} %get-tuple-element.11), channel_id=1, source_target_pairs={{16,0},{17,1},{18,2},{19,3},{20,4},{21,5},{22,6},{23,7},{24,8},{25... | collective-permute-start | bytes 196616 | tf_op jit(solution)/shard_map/ppermute | solution.py:222
  20.9 10.0 %collective-permute-start.2 = (f32[32,8,128]{2,1,0:T(8,128)S(1)}, f32[32,8,128]{2,1,0:T(8,128)S(1)}, u32[]{:S(2)}, u32[]{:S(2)}) collective-permute-start(f32[32,8,128]{2,1,0:T(8,128)S(1)} %get-tuple-element.6), channel_id=1, source_target_pairs={{0,1},{1,2},{2,3},{3,4},{4,5},{5,6},{6,7},{7,8},{8,9},{9,10},{10,1... | collective-permute-start | bytes 393224 | tf_op jit(solution)/shard_map/ppermute | solution.py:221
  25.4 6.9 %collective-permute-start.3 = (f32[32,8,128]{2,1,0:T(8,128)S(1)}, f32[32,8,128]{2,1,0:T(8,128)S(1)}, u32[]{:S(2)}, u32[]{:S(2)}) collective-permute-start(f32[32,8,128]{2,1,0:T(8,128)S(1)} %get-tuple-element.7), channel_id=1, source_target_pairs={{1,0},{2,1},{3,2},{4,3},{5,4},{6,5},{7,6},{8,7},{9,8},{10,9},{11,1... | collective-permute-start | bytes 393224 | tf_op jit(solution)/shard_map/ppermute | solution.py:222
  27.3 5.0 %copy-start = (f32[16,16,128]{2,1,0:T(8,128)S(1)}, f32[16,16,128]{2,1,0:T(8,128)}, u32[]{:S(2)}) copy-start(f32[16,16,128]{2,1,0:T(8,128)} %precond_ref.3) | copy-start | bytes 393220
  27.3 5.0 %copy-start.1 = (f32[16,16,128]{2,1,0:T(8,128)S(1)}, f32[16,16,128]{2,1,0:T(8,128)}, u32[]{:S(2)}) copy-start(f32[16,16,128]{2,1,0:T(8,128)} %data_ref.3) | copy-start | bytes 393220
  27.3 5.0 %copy-start.2 = (f32[256,128]{1,0:T(8,128)S(1)}, f32[256,128]{1,0:T(8,128)}, u32[]{:S(2)}) copy-start(f32[256,128]{1,0:T(8,128)} %constant.24.clone.back_ref) | copy-start | bytes 393220
  27.4 5.0 %copy-start.3 = (f32[128,256]{1,0:T(8,128)S(1)}, f32[128,256]{1,0:T(8,128)}, u32[]{:S(2)}) copy-start(f32[128,256]{1,0:T(8,128)} %constant.23.clone.field_ref) | copy-start | bytes 393220
  39.7 2.6 %collective-permute-start.6 = (f32[8,16,128]{2,1,0:T(8,128)S(1)}, f32[8,16,128]{2,1,0:T(8,128)S(1)}, u32[]{:S(2)}, u32[]{:S(2)}) collective-permute-start(f32[8,16,128]{2,1,0:T(8,128)S(1)} %get-tuple-element.9), channel_id=1, source_target_pairs={{0,16},{1,17},{2,18},{3,19},{4,20},{5,21},{6,22},{7,23},{8,24},{9,... | collective-permute-start | bytes 196616 | tf_op jit(solution)/shard_map/ppermute | solution.py:221
  41.0 3.1 %collective-permute-start.7 = (f32[8,16,128]{2,1,0:T(8,128)S(1)}, f32[8,16,128]{2,1,0:T(8,128)S(1)}, u32[]{:S(2)}, u32[]{:S(2)}) collective-permute-start(f32[8,16,128]{2,1,0:T(8,128)S(1)} %get-tuple-element.8), channel_id=1, source_target_pairs={{16,0},{17,1},{18,2},{19,3},{20,4},{21,5},{22,6},{23,7},{24,8},{25... | collective-permute-start | bytes 196616 | tf_op jit(solution)/shard_map/ppermute | solution.py:222
  44.2 7.7 %collective-permute-start.8 = (f32[32,8,128]{2,1,0:T(8,128)S(1)}, f32[32,8,128]{2,1,0:T(8,128)S(1)}, u32[]{:S(2)}, u32[]{:S(2)}) collective-permute-start(f32[32,8,128]{2,1,0:T(8,128)S(1)} %get-tuple-element.4), channel_id=1, source_target_pairs={{0,1},{1,2},{2,3},{3,4},{4,5},{5,6},{6,7},{7,8},{8,9},{9,10},{10,1... | collective-permute-start | bytes 393224 | tf_op jit(solution)/shard_map/ppermute | solution.py:221
  48.8 7.4 %collective-permute-start.9 = (f32[32,8,128]{2,1,0:T(8,128)S(1)}, f32[32,8,128]{2,1,0:T(8,128)S(1)}, u32[]{:S(2)}, u32[]{:S(2)}) collective-permute-start(f32[32,8,128]{2,1,0:T(8,128)S(1)} %get-tuple-element.5), channel_id=1, source_target_pairs={{1,0},{2,1},{3,2},{4,3},{5,4},{6,5},{7,6},{8,7},{9,8},{10,9},{11,1... | collective-permute-start | bytes 393224 | tf_op jit(solution)/shard_map/ppermute | solution.py:222
where the time goes:
time: 64.1 us; the launch traced here: 63.7 us
  starting transfers between devices  20.3 us (32%)
  waiting for transfers between devices  18 us (28%)
  Pallas kernels  18 us (28%)
  other arithmetic  5.06 us (8%)
  local copies, waits for them, and re-layouts  1.39 us (2%)
  between operations  0.98 us (2%)
    pallas_call x2, Pallas kernels, local(): model, residual = apply(region, data, precond, spectra, field, back)  14.6 us
    ppermute x4, starting transfers between devices, padded_2(): before = lax.ppermute(last, axis, up)  12.5 us
    ppermute x2, waiting for transfers between devices, passed_along(): return lax.ppermute(shard, axis, pairs)  8.58 us
    ppermute x4, waiting for transfers between devices, padded_2(): after = lax.ppermute(leading, axis, down)  7.65 us
    ppermute x4, starting transfers between devices, padded_2(): after = lax.ppermute(leading, axis, down)  5.17 us
    pallas_call x1, Pallas kernels, local(): pl.pallas_call(functools.partial(spectra_kernel, width, region_x, region_...  3.32 us
    ppermute x2, starting transfers between devices, passed_along(): return lax.ppermute(shard, axis, pairs)  2.58 us
    ppermute x4, waiting for transfers between devices, padded_2(): before = lax.ppermute(last, axis, up)  1.76 us
  transfers between devices with their start and end apart: 10, of which 6 were waited for; matrix products, arithmetic and copies ran while one was open for 5% of the time, Pallas kernels for 5%

commit v1 on v0

v1 whole, which is shorter than its diff:
```python
import functools
import math

import jax
import jax.numpy as jnp
import numpy as np
from jax import lax
from jax.experimental import pallas as pl
from jax.experimental.pallas import tpu as pltpu
from jax.sharding import PartitionSpec as P

ITERS = 2
relaxation = 0.7
LANES = 128
SUB = 8


def times_phase(value, turn, size, sign):
    if value is None:
        return None
    re, im = value
    turn = (sign * turn) % size
    eighth = 8 * turn
    if eighth == 0:
        return value
    if eighth == 2 * size:
        return (-im, re)
    if eighth == 4 * size:
        return (-re, -im)
    if eighth == 6 * size:
        return (im, -re)
    angle = 2.0 * math.pi * turn / size
    cosine, sine = math.cos(angle), math.sin(angle)
    if eighth % size == 0:
        root = math.sqrt(0.5)
        first, second = (re - im) * root, (re + im) * root
        if eighth == size:
            return (first, second)
        if eighth == 3 * size:
            return (-second, first)
        if eighth == 5 * size:
            return (-first, -second)
        return (second, -first)
    return (re * cosine - im * sine, re * sine + im * cosine)


def plus(a, b):
    if a is None:
        return b
    if b is None:
        return a
    return (a[0] + b[0], a[1] + b[1])


def minus(a, b):
    if b is None:
        return a
    if a is None:
        return (-b[0], -b[1])
    return (a[0] - b[0], a[1] - b[1])


def transform(values, sign, wanted):
    size = len(values)
    if all(v is None for v in values):
        return [None] * wanted
    if size == 1:
        return list(values)
    half = size // 2
    if size % 2:
        raise ValueError("length")
    even = transform(values[0::2], sign, min(half, wanted))
    odd = transform(values[1::2], sign, min(half, wanted))
    odd = [times_phase(v, k, size, sign) for k, v in enumerate(odd)]
    low = [plus(a, b) for a, b in zip(even, odd)]
    high = [minus(a, b) for a, b in zip(even, odd)]
    return (low + high)[:wanted]


def tables(depth, width):
    half = width // 2
    length = depth + 2 * half
    count = length // 2 + 1
    k = np.arange(count)
    field = np.zeros((depth, 2 * LANES))
    turns = (np.arange(depth)[:, None] + half) * k[None, :] % length
    angle = turns * (2.0 * np.pi / length)
    field[:, :count] = np.cos(angle)
    field[:, LANES : LANES + count] = -np.sin(angle)
    kernel = np.zeros((LANES, 2 * LANES))
    angle = np.arange(width)[:, None] * k[None, :] % length * (2.0 * np.pi / length)
    kernel[:width, :count] = np.cos(angle)
    kernel[:width, LANES : LANES + count] = np.sin(angle)
    back = np.zeros((2 * LANES, depth))
    weight = np.where((k == 0) | (2 * k == length), 1.0, 2.0) / length
    angle = k[:, None] * np.arange(depth)[None, :] % length * (2.0 * np.pi / length)
    back[:count] = weight[:, None] * np.cos(angle)
    back[LANES : LANES + count] = -weight[:, None] * np.sin(angle)
    return field, kernel, back


def stacked(table):
    high = jnp.asarray(table, jnp.float32).astype(jnp.bfloat16)
    low = (jnp.asarray(table, jnp.float32) - high.astype(jnp.float32)).astype(jnp.bfloat16)
    return jnp.concatenate([high, high, low])


def product(left, table):
    high = left.astype(jnp.bfloat16)
    low = (left - high.astype(jnp.float32)).astype(jnp.bfloat16)
    left = jnp.concatenate([high, low, high], axis=1)
    return jnp.dot(left, table, preferred_element_type=jnp.float32)


def pitch_of(rows):
    return rows + SUB if rows % (4 * SUB) == 0 else rows


def spectra(width, region_x, region_y, rows, packed, table_ref, g_ref, k1r, k1i, k2r, k2i):
    lanes = packed.shape[1]
    for b in range(width):
        shifted = packed[...]
        if b:
            shifted = pltpu.roll(shifted, lanes - b * width, axis=1)
        both = product(shifted[:, :LANES], table_ref[...])
        k1r[pl.ds(b * rows, rows), :] = both[:, :LANES]
        k1i[pl.ds(b * rows, rows), :] = both[:, LANES:]

    @pl.loop(0, rows // SUB)
    def _(tile):
        at = lambda i: pl.ds(pl.multiple_of(i * rows + tile * SUB, SUB), SUB)
        values = [(k1r[at(b), :], k1i[at(b), :]) for b in range(width)]
        values += [None] * (region_y - width)
        for ky, (re, im) in enumerate(transform(values, 1, region_y)):
            k2r[at(ky), :] = re
            k2i[at(ky), :] = im

    @pl.loop(0, 4)
    def _(node):
        @pl.loop(0, region_y // SUB)
        def _(tile):
            at = lambda a: pl.ds(tile * SUB * rows + node * width + a, SUB, stride=rows)
            values = [(k2r[at(a), :], k2i[at(a), :]) for a in range(width)]
            values += [None] * (region_x - width)
            for kx, (re, im) in enumerate(transform(values, 1, region_x)):
                to = pl.ds(pl.multiple_of(kx * region_y + tile * SUB, SUB), SUB)
                g_ref[node, 0, to, :] = re
                g_ref[node, 1, to, :] = im


def depth_forward(region, box, field_ref, zr, zi, pitch):
    x0, nx, y0, ny = box
    step = max(1, 2 * LANES // ny)
    for x in range(x0, x0 + nx, step):
        count = min(step, x0 + nx - x)
        left = region[pl.ds(x, count), pl.ds(y0, ny), :].reshape(count * ny, LANES)
        both = product(left, field_ref[...])
        for i in range(count):
            zr[pl.ds((x + i) * pitch + y0, ny), :] = both[i * ny : (i + 1) * ny, :LANES]
            zi[pl.ds((x + i) * pitch + y0, ny), :] = both[i * ny : (i + 1) * ny, LANES:]


def blended_columns(
    count_x, count_y, half, g_ref, back_ref, zr, zi, yr, yi, vx, ur, ui, w_ref, o_ref
):
    region_x, region_y = count_x + 2 * half, count_y + 2 * half
    pitch_x, pitch_y = pitch_of(region_x), pitch_of(region_y)

    @pl.loop(0, region_x // SUB)
    def _(tile):
        at = lambda y: pl.ds(tile * SUB * pitch_y + y, SUB, stride=pitch_y)
        values = [(zr[at(y), :], zi[at(y), :]) for y in range(region_y)]
        for ky, (re, im) in enumerate(transform(values, -1, region_y)):
            to = pl.ds(pl.multiple_of(ky * pitch_x + tile * SUB, SUB), SUB)
            yr[to, :] = re
            yi[to, :] = im

    @pl.loop(0, region_y // SUB)
    def _(tile):
        at = lambda x: pl.ds(tile * SUB * pitch_x + x, SUB, stride=pitch_x)
        values = [(yr[at(x), :], yi[at(x), :]) for x in range(region_x)]
        for kx, (re, im) in enumerate(transform(values, -1, region_x)):
            vx[0, kx] = re
            vx[1, kx] = im

        @pl.loop(0, 2)
        def _(j):
            parts = []
            for i in range(2):
                values = []
                for kx in range(region_x):
                    to = pl.ds(pl.multiple_of(kx * region_y + tile * SUB, SUB), SUB)
                    gr, gi = g_ref[2 * j + i, 0, to, :], g_ref[2 * j + i, 1, to, :]
                    vr, vi = vx[0, kx], vx[1, kx]
                    values.append((vr * gr - vi * gi, vr * gi + vi * gr))
                parts.append(transform(values, 1, count_x))
            for x in range(count_x):
                s = (x + 0.5) / count_x
                to = pl.ds(pl.multiple_of(x * pitch_y + tile * SUB, SUB), SUB)
                (ar, ai), (br, bi) = parts[0][x], parts[1][x]
                ur[j, to, :] = (1.0 - s) * ar + s * br
                ui[j, to, :] = (1.0 - s) * ai + s * bi

    @pl.loop(0, count_x // SUB)
    def _(tile):
        parts = []
        for j in range(2):
            at = lambda ky: pl.ds(tile * SUB * pitch_y + ky, SUB, stride=pitch_y)
            values = [(ur[j, at(ky), :], ui[j, at(ky), :]) for ky in range(region_y)]
            parts.append(transform(values, 1, count_y))
        for y in range(count_y):
            t = (y + 0.5) / count_y
            to = pl.ds(pl.multiple_of(y * count_x + tile * SUB, SUB), SUB)
            (ar, ai), (br, bi) = parts[0][y], parts[1][y]
            w_ref[to, :LANES] = (1.0 - t) * ar + t * br
            w_ref[to, LANES:] = (1.0 - t) * ai + t * bi

    o_ref[...] = product(w_ref[...], back_ref[...])


class Link:
    def __init__(self, sems, k, src, dst, axis, by, only=True):
        here, size = lax.axis_index(axis), lax.axis_size(axis)
        inside = lambda i: jnp.logical_and(jnp.logical_and(i >= 0, i < size), only)
        self.sends, self.gets = inside(here + by), inside(here - by)
        self.copy = pltpu.make_async_remote_copy(
            src_ref=src, dst_ref=dst, send_sem=sems[0].at[k], recv_sem=sems[1].at[k],
            device_id={axis: here + by}, device_id_type=pl.DeviceIdType.MESH,
        )

    def start(self):
        pl.when(self.sends)(lambda: self.copy.start())

    def wait_recv(self):
        pl.when(self.gets)(lambda: self.copy.wait_recv())

    def wait_send(self):
        pl.when(self.sends)(lambda: self.copy.wait_send())


def halo_links(region, count_x, count_y, half, sems, base):
    gy, size = lax.axis_index("gy"), lax.axis_size("gy")
    own_x, own_y = pl.ds(half, count_x), pl.ds(half, count_y)
    low, high_x, high_y = pl.ds(0, half), pl.ds(half + count_x, half), pl.ds(half + count_y, half)
    last_x, last_y, first = pl.ds(count_x, half), pl.ds(count_y, half), pl.ds(half, half)
    at = lambda x, y: region.at[x, y]
    along_y = [
        Link(sems, base, at(own_x, last_y), at(own_x, low), "gy", 1),
        Link(sems, base + 1, at(own_x, first), at(own_x, high_y), "gy", -1),
    ]
    along_x = [
        Link(sems, base + 2, at(last_x, own_y), at(low, own_y), "gx", 1),
        Link(sems, base + 3, at(first, own_y), at(high_x, own_y), "gx", -1),
    ]
    relayed = [
        Link(sems, base + 4, at(last_x, low), at(low, low), "gx", 1, gy > 0),
        Link(sems, base + 5, at(first, low), at(high_x, low), "gx", -1, gy > 0),
        Link(sems, base + 6, at(last_x, high_y), at(low, high_y), "gx", 1, gy < size - 1),
        Link(sems, base + 7, at(first, high_y), at(high_x, high_y), "gx", -1, gy < size - 1),
    ]
    return along_y, along_x, relayed


def whole_kernel(
    count_x, count_y, half, rows,
    data_ref, precond_ref, psf_ref, field_ref, kernel_ref, back_ref,
    model_ref, residual_ref,
    region0, region1, nodes, packed, g_ref, k1r, k1i, k2r, k2i,
    zr, zi, yr, yi, vx, ur, ui, w_ref, o_ref, send_sem, recv_sem,
):
    width = 2 * half + 1
    region_x, region_y = count_x + 2 * half, count_y + 2 * half
    pitch_y = pitch_of(region_y)
    sems = (send_sem, recv_sem)
    gx, gy = lax.axis_index("gx"), lax.axis_index("gy")
    size_x, size_y = lax.axis_size("gx"), lax.axis_size("gy")
    regions = [region0, region1]
    for region in regions:
        region[...] = jnp.zeros(region.shape, region.dtype)

    barrier = pltpu.get_barrier_semaphore()
    for axis, here, size in (("gx", gx, size_x), ("gy", gy, size_y)):
        for by in (-1, 1):
            @pl.when(jnp.logical_and(here + by >= 0, here + by < size))
            def _():
                pl.semaphore_signal(
                    barrier, inc=1, device_id={axis: here + by},
                    device_id_type=pl.DeviceIdType.MESH,
                )

    own = (pl.ds(half, count_x), pl.ds(half, count_y))
    region0[own] = precond_ref[...] * data_ref[...]
    peers = 0
    for here, size in ((gx, size_x), (gy, size_y)):
        peers += (here > 0).astype(jnp.int32) + (here < size - 1).astype(jnp.int32)
    pl.semaphore_wait(barrier, peers)

    inline = Link(sems, 16, psf_ref, nodes.at[0], "gx", -1)
    crossline = Link(sems, 17, psf_ref, nodes.at[1], "gy", -1)
    corner = Link(sems, 18, nodes.at[1], nodes.at[2], "gx", -1, gy < size_y - 1)
    crossline.start()
    inline.start()
    started = [crossline, inline, corner]

    for sweep_index in range(ITERS):
        region = regions[sweep_index]
        along_y, along_x, relayed = halo_links(
            region, count_x, count_y, half, sems, 8 * sweep_index
        )
        started += along_y + along_x + relayed
        for link in along_y + along_x:
            link.start()
        depth_forward(region, (half, count_x, half, count_y), field_ref, zr, zi, pitch_y)
        if sweep_index == 0:
            crossline.wait_recv()
            corner.start()
            inline.wait_recv()
            corner.wait_recv()
            last_x, last_y = gx == size_x - 1, gy == size_y - 1
            part = lambda n: pl.ds(n * width, width)

            def fill(n, edge, other, slot):
                @pl.when(edge)
                def _():
                    packed[part(n), :] = packed[part(other), :]

                @pl.when(jnp.logical_not(edge))
                def _():
                    packed[part(n), :] = nodes[slot, pl.ds(0, width), :]

            packed[...] = jnp.zeros(packed.shape, packed.dtype)
            packed[part(0), :] = psf_ref[pl.ds(0, width), :]
            fill(1, last_x, 0, 0)
            fill(2, last_y, 0, 1)

            @pl.when(last_x)
            def _():
                packed[part(3), :] = packed[part(2), :]

            @pl.when(jnp.logical_not(last_x))
            def _():
                fill(3, last_y, 1, 2)

            spectra(
                width, region_x, region_y, rows, packed, kernel_ref, g_ref, k1r, k1i, k2r, k2i
            )
        for link in along_y:
            link.wait_recv()
        for link in relayed:
            link.start()
        depth_forward(region, (half, count_x, 0, half), field_ref, zr, zi, pitch_y)
        depth_forward(region, (half, count_x, half + count_y, half), field_ref, zr, zi, pitch_y)
        for link in along_x + relayed:
            link.wait_recv()
        depth_forward(region, (0, half, 0, region_y), field_ref, zr, zi, pitch_y)
        depth_forward(region, (half + count_x, half, 0, region_y), field_ref, zr, zi, pitch_y)
        blended_columns(
            count_x, count_y, half, g_ref, back_ref, zr, zi, yr, yi, vx, ur, ui, w_ref, o_ref
        )
        last = sweep_index == ITERS - 1
        for x in range(count_x):
            blended = o_ref[pl.ds(x, count_y, stride=count_x), :]
            model = region[x + half, pl.ds(half, count_y), :]
            residual = data_ref[x] - (model + blended)
            model = model + relaxation * precond_ref[x] * residual
            if last:
                residual_ref[x] = residual
                model_ref[x] = model
            else:
                regions[sweep_index + 1][x + half, pl.ds(half, count_y), :] = model
    for link in started:
        link.wait_send()


def local(data, precond, psf):
    count_x, count_y, depth = data.shape
    width = psf.shape[2]
    half = width // 2
    region_x, region_y = count_x + 2 * half, count_y + 2 * half
    pitch_x, pitch_y = pitch_of(region_x), pitch_of(region_y)
    field, kernel, back = tables(depth, width)
    back = back / (region_x * region_y)
    f32 = jnp.float32
    up = lambda n, m: -(-n // m) * m
    flat = psf.reshape(width, width * width)
    high, lanes = up(width, SUB), up(width * width, LANES)
    flat = jnp.pad(flat, ((0, high - width), (0, lanes - width * width)))
    rows = up(4 * width, SUB)
    vmem = lambda *shape: pltpu.VMEM(shape, f32)
    square = region_x * region_y
    spec = pl.BlockSpec(memory_space=pltpu.VMEM)
    model, residual = pl.pallas_call(
        functools.partial(whole_kernel, count_x, count_y, half, rows),
        out_shape=[jax.ShapeDtypeStruct(data.shape, f32)] * 2,
        in_specs=[spec] * 6,
        out_specs=[spec] * 2,
        scratch_shapes=[
            vmem(region_x, region_y, depth),
            vmem(region_x, region_y, depth),
            vmem(3, high, lanes),
            vmem(rows, lanes),
            vmem(4, 2, square, LANES),
            vmem(width * rows, LANES),
            vmem(width * rows, LANES),
            vmem(region_y * rows, LANES),
            vmem(region_y * rows, LANES),
            vmem(region_x * pitch_y, LANES),
            vmem(region_x * pitch_y, LANES),
            vmem(region_y * pitch_x, LANES),
            vmem(region_y * pitch_x, LANES),
            vmem(2, region_x, SUB, LANES),
            vmem(2, count_x * pitch_y, LANES),
            vmem(2, count_x * pitch_y, LANES),
            vmem(count_x * count_y, 2 * LANES),
            vmem(count_x * count_y, LANES),
            pltpu.SemaphoreType.DMA((19,)),
            pltpu.SemaphoreType.DMA((19,)),
        ],
        compiler_params=pltpu.CompilerParams(
            vmem_limit_bytes=32 << 20, collective_id=0, has_side_effects=True
        ),
        name="whole",
    )(data, precond, flat, stacked(field), stacked(kernel), stacked(back))
    return model, residual


def solution(mesh):
    placed = (P("gx", "gy", None), P("gx", "gy", None), P("gx", "gy", None, None, None))
    return jax.shard_map(
        local,
        mesh=mesh,
        in_specs=placed,
        out_specs=(P("gx", "gy", None), P("gx", "gy", None)),
        check_vma=False,
    )
```

time: 64.1 us -> 31.8 us (0.50)
  starting transfers between devices: 20.3 us -> 0 us
  waiting for transfers between devices: 18 us -> 0 us
  Pallas kernels: 18 us -> 25.5 us
  other arithmetic: 5.06 us -> 1.34 us
  local copies, waits for them, and re-layouts: 1.39 us -> 4.02 us
    ppermute x10 -> x0, starting transfers between devices: 20.3 us -> none  [the longest x4 12.5 us: padded_2(): before = lax.ppermute(last, axis, up)]
    ppermute x10 -> x0, waiting for transfers between devices: 18 us -> none  [the longest x2 8.58 us: passed_along(): return lax.ppermute(shard, axis, pairs)]
    pallas_call x3 -> x1, Pallas kernels: 18 us -> 25.5 us  [local(): pl.pallas_call(functools.partial(whole_kernel, count_x, count_y, half, ro...]
    unnamed x17 -> x12, local copies, waits for them, and re-layouts: 1.18 us -> 3.9 us
    select_n x2 -> x0, other arithmetic: 2.23 us -> none  [the longest x1 1.29 us: node_kernels(): crossline = jnp.where(last_crossline, pair, passed_along(pair, 'gy', -1))]
    unnamed x0 -> x1, other arithmetic: none -> 1.34 us
    another operation x1 -> x0, other arithmetic: 1.25 us -> none  [node_kernels(): pair = jnp.stack([own, inline])]
    mul x1 -> x0, other arithmetic: 0.99 us -> none  [local(): model = precond * data]
  transfers between devices with their start and end apart: 10 -> 0, of which waited for: 6 -> 0; matrix products, arithmetic and copies ran while one was open for 5% -> 0% of each run, Pallas kernels for 5% -> 0%
where the time goes in v1:
time: 31.8 us; the launch traced here: 31.6 us
  Pallas kernels  25.5 us (80%)
  local copies, waits for them, and re-layouts  4.02 us (13%)
  other arithmetic  1.34 us (4%)
  between operations  0.69 us (2%)
    pallas_call x1, Pallas kernels, local(): pl.pallas_call(functools.partial(whole_kernel, count_x, count_y, half, ro...  25.5 us
    unnamed x12, local copies, waits for them, and re-layouts  3.9 us
    unnamed x1, other arithmetic  1.34 us

profile of v1, /device:TPU:0, one launch (start us, length us, event | category | flops | bytes accessed | tf_op | source)
XLA Modules:
  0.0 31.6 jit_solution(11749147564369278057)
XLA Ops:
  0.6 0.0 copy-start.1
  0.6 0.0 copy-start.2
  0.7 1.3 %reduce = f32[17,17,17]{2,1,0:T(8,128)S(1)} reduce(f32[1,1,17,17,17]{4,1,3,2,0:T(1,128)} %param.11, f32[]{:T(128)} %constant.30), dimensions={0,1}, to_apply=%param.11.reduce_sub_computation | reduce | bytes 39308 | tf_op args[2]
  2.0 0.0 copy-start
  2.0 0.1 reshape.7
  2.1 0.0 copy-done.1
  2.2 0.0 copy-done.2
  2.2 0.8 %copy-done = bf16[768,128]{1,0:T(8,128)(2,1)S(1)} copy-done((bf16[768,128]{1,0:T(8,128)(2,1)S(1)}, bf16[768,128]{1,0:T(8,128)(2,1)}, u32[]{:S(2)}) %copy-start) | copy-done | bytes 196632
  2.9 0.0 copy-start.3
  2.9 0.9 %copy-done.3 = f32[16,16,128]{2,1,0:T(8,128)S(1)} copy-done((f32[16,16,128]{2,1,0:T(8,128)S(1)}, f32[16,16,128]{2,1,0:T(8,128)}, u32[]{:S(2)}) %copy-start.3) | copy-done | bytes 131096
  3.8 0.0 copy-start.4
  3.8 0.9 %copy-done.4 = f32[16,16,128]{2,1,0:T(8,128)S(1)} copy-done((f32[16,16,128]{2,1,0:T(8,128)S(1)}, f32[16,16,128]{2,1,0:T(8,128)}, u32[]{:S(2)}) %copy-start.4) | copy-done | bytes 131096
  4.7 25.5 %whole.1 = (f32[16,16,128]{2,1,0:T(8,128)S(1)}, f32[16,16,128]{2,1,0:T(8,128)S(1)}) custom-call(f32[16,16,128]{2,1,0:T(8,128)S(1)} %copy-done.3, f32[16,16,128]{2,1,0:T(8,128)S(1)} %copy-done.4, f32[24,384]{1,0:T(8,128)S(1)} %pad.4.psf_ref, bf16[384,256]{1,0:T(8,128)(2,1)S(1)} %copy-done.2, bf16[384,256]{1,0:T(8,128)(2,1)S(1)} %copy-done.1, ...), custom_call_target="tpu_custom_call" | custom-call | tf_op jit(solution)/shard_map/whole/pallas_call | solution.py:392
  30.2 0.7 %copy.13 = f32[16,16,128]{2,1,0:T(8,128)} copy(f32[16,16,128]{2,1,0:T(8,128)S(1)} %get-tuple-element.4) | data formatting | bytes 262144
  30.9 0.7 %copy.14 = f32[16,16,128]{2,1,0:T(8,128)} copy(f32[16,16,128]{2,1,0:T(8,128)S(1)} %get-tuple-element.5) | data formatting | bytes 262144
  (1 shorter events, 0.0 us)
Async XLA Ops:
  0.6 1.5 %copy-start.1 = (bf16[384,256]{1,0:T(8,128)(2,1)S(1)}, bf16[384,256]{1,0:T(8,128)(2,1)}, u32[]{:S(2)}) copy-start(bf16[384,256]{1,0:T(8,128)(2,1)} %constant.24.kernel_ref) | copy-start | bytes 589828
  0.6 1.5 %copy-start.2 = (bf16[384,256]{1,0:T(8,128)(2,1)S(1)}, bf16[384,256]{1,0:T(8,128)(2,1)}, u32[]{:S(2)}) copy-start(bf16[384,256]{1,0:T(8,128)(2,1)} %constant.19.field_ref) | copy-start | bytes 589828
  2.0 0.9 %copy-start = (bf16[768,128]{1,0:T(8,128)(2,1)S(1)}, bf16[768,128]{1,0:T(8,128)(2,1)}, u32[]{:S(2)}) copy-start(bf16[768,128]{1,0:T(8,128)(2,1)} %constant.29.back_ref) | copy-start | bytes 589828
  2.9 0.9 %copy-start.3 = (f32[16,16,128]{2,1,0:T(8,128)S(1)}, f32[16,16,128]{2,1,0:T(8,128)}, u32[]{:S(2)}) copy-start(f32[16,16,128]{2,1,0:T(8,128)} %data_ref.1) | copy-start | bytes 393220
  3.8 0.9 %copy-start.4 = (f32[16,16,128]{2,1,0:T(8,128)S(1)}, f32[16,16,128]{2,1,0:T(8,128)}, u32[]{:S(2)}) copy-start(f32[16,16,128]{2,1,0:T(8,128)} %precond_ref.1) | copy-start | bytes 393220
